TPU v7x, 32 devices: a whole 2x2x4 slice. The times are simulated.
32 devices in a mesh: groups: 2 (over y), ep: 16 (over z, x, core).
Axes of the slice: x: 2, y: 2, z: 4, core: 2. Of those that a mesh axis runs over, the one named last changes fastest.
Arguments:
- tokens: bfloat16 [128, 7168], P(('groups', 'ep')), parts along dimension 0, may hold values from -6 to 6
- routes: int32 [128, 8], P(('groups', 'ep')), parts along dimension 0, may hold values from 0 to 15, as said below
- gates: float32 [128, 8], P(('groups', 'ep')), parts along dimension 0, may hold values from 0.05 to 0.6
- gate_weight: bfloat16 [7168, 32768], P(None, 'ep'), may hold values from -0.0625 to 0.0625
- up_weight: bfloat16 [7168, 32768], P(None, 'ep'), may hold values from -0.0625 to 0.0625
- down_weight: bfloat16 [32768, 7168], P('ep'), may hold values from -0.125 to 0.125
Outputs:
- mixed: bfloat16 [128, 7168], P(('groups', 'ep')), parts along dimension 0
There are 2 independent parts, one for each index of `groups`. A program takes and returns all parts, laid end to end along the dimension named above; an argument that names none is the same for every part. Nothing has to cross between parts.
Inputs may be any that keep to these rules, and one draw needn't show every extreme that they name: `routes`: each token names 8 different experts. Among the 4 tokens of one device no expert is named by more than 3 of them, and in every draw one expert is named by exactly 3 tokens of every device.
All inputs are finite; a program needn't handle non-finite values.
Results may differ from a plain program's by a relative error of at most 0.0085.
Values may be sent and summed in bfloat16 or wider, within the bound.
A program may use at most 128 MiB of HBM per device.

v0:
```python
import functools

import jax
import jax.numpy as jnp
from jax import lax
from jax.experimental import pallas as pl
from jax.experimental.pallas import tpu as pltpu
from jax.sharding import PartitionSpec as P

EXPERTS = 16
SLOTS = 3
AUX = 128


def piece(total, want):
    size = want
    while total % size:
        size //= 2
    return size


def kernel(
    devices, kc, nc, tile,
    tokens, routes, gates, wg, wu, wd, out,
    ring_g, ring_u, down, rx, ax, xf, xb, acc_g, acc_u, hid, share, mine, theirs, sbuf, rbuf,
    tok_sem, g_sem, u_sem, d_sem,
    tx_send, tx_recv, re_send, re_recv, ob_send, ob_recv, rt_send, rt_recv, ax_send, ax_recv,
):
    rows, width = tokens.shape
    hidden = wg.shape[1]
    chips = devices // 2
    units, outs = width // kc, width // nc
    me = lax.axis_index("ep")
    chip, core = me // 2, me % 2
    other = 1 - core
    peer = chip * 2 + other
    mates = chips * rows

    def remote(src, dst, send, recv, dev):
        return pltpu.make_async_remote_copy(
            src_ref=src, dst_ref=dst, send_sem=send, recv_sem=recv,
            device_id={"ep": dev}, device_id_type=pl.DeviceIdType.MESH,
        )

    def load_tokens(j):
        return pltpu.make_async_copy(
            tokens.at[:, pl.ds(j * kc, kc)], rx.at[j, core, chip], tok_sem.at[j]
        )

    def load_g(j):
        s = j % SLOTS
        return pltpu.make_async_copy(wg.at[pl.ds(j * kc, kc), :], ring_g.at[s], g_sem.at[s])

    def load_u(j):
        s = j % SLOTS
        return pltpu.make_async_copy(wu.at[pl.ds(j * kc, kc), :], ring_u.at[s], u_sem.at[s])

    def load_d(c):
        return pltpu.make_async_copy(wd.at[:, pl.ds(c * nc, nc)], down.at[c], d_sem.at[c])

    for j in range(units):
        load_tokens(j).start()
    for j in range(min(SLOTS, units)):
        load_g(j).start()
        load_u(j).start()
    issued = min(2, outs)
    for c in range(issued):
        load_d(c).start()

    barrier = pltpu.get_barrier_semaphore()
    pl.semaphore_signal(barrier, inc=1, device_id={"ep": peer}, device_id_type=pl.DeviceIdType.MESH)

    @pl.loop(1, chips)
    def _(i):
        to = lax.rem(chip + i, chips) * 2 + core
        pl.semaphore_signal(barrier, inc=1, device_id={"ep": to}, device_id_type=pl.DeviceIdType.MESH)

    lane = lax.broadcasted_iota(jnp.int32, (rows, AUX), 1)
    name = jnp.where(lane < EXPERTS, lane, lane - EXPERTS)
    weight = jnp.zeros((rows, AUX), jnp.float32)
    for k in range(routes.shape[1]):
        weight = weight + jnp.where(routes[:, k : k + 1] == name, gates[:, k : k + 1], 0.0)
    high = weight.astype(jnp.bfloat16).astype(jnp.float32)
    ax[core, chip] = jnp.where(
        lane < EXPERTS, high, jnp.where(lane < 2 * EXPERTS, weight - high, 0.0)
    ).astype(jnp.bfloat16)

    pl.semaphore_wait(barrier, chips)

    for j in range(units):
        load_tokens(j).wait()

        @pl.loop(1, chips)
        def _(i):
            to = lax.rem(chip + i, chips) * 2 + core
            remote(rx.at[j, core, chip], rx.at[j, core, chip], tx_send.at[j], tx_recv.at[j], to).start()

    @pl.loop(1, chips)
    def _(i):
        to = lax.rem(chip + i, chips) * 2 + core
        remote(ax.at[core, chip], ax.at[core, chip], ax_send.at[0], ax_recv.at[0], to).start()

    def many(ref, sem):
        return pltpu.make_async_copy(ref, ref, sem)

    def relay(j):
        return remote(rx.at[j, core], rx.at[j, core], re_send.at[j], re_recv.at[j], peer)

    relay_aux = remote(ax.at[core], ax.at[core], ax_send.at[1], ax_recv.at[1], peer)

    def forward(j):
        many(rx.at[j, 0, pl.ds(0, chips - 1)], tx_recv.at[j]).wait()
        relay(j).start()

    forward(0)
    for j in range(units):
        if j + 1 < units:
            forward(j + 1)
        else:
            many(ax.at[0, pl.ds(0, chips - 1)], ax_recv.at[0]).wait()
            relay_aux.start()
        relay(j).wait_recv()
        for half in range(2):
            @pl.loop(0, chips // 2)
            def _(b):
                pair = jnp.concatenate(
                    [rx[j, half, 2 * b].astype(jnp.float32), rx[j, half, 2 * b + 1].astype(jnp.float32)], axis=0
                )
                at = pl.multiple_of(half * mates + b * 2 * rows, 2 * rows)
                xf[pl.ds(at, 2 * rows), :] = pair
        xb[...] = xf[...].astype(jnp.bfloat16)
        load_g(j).wait()
        load_u(j).wait()
        s = j % SLOTS

        @pl.loop(0, hidden // tile, unroll=True)
        def _(n):
            cols = pl.ds(pl.multiple_of(n * tile, tile), tile)
            pg = jnp.dot(xb[...], ring_g[s, :, cols], preferred_element_type=jnp.float32)
            pu = jnp.dot(xb[...], ring_u[s, :, cols], preferred_element_type=jnp.float32)
            if j == 0:
                acc_g[:, cols] = pg
                acc_u[:, cols] = pu
            elif j < units - 1:
                acc_g[:, cols] += pg
                acc_u[:, cols] += pu
            else:
                g = acc_g[:, cols] + pg
                u = acc_u[:, cols] + pu
                hid[:, cols] = (g / (1.0 + jnp.exp(-g)) * u).astype(jnp.bfloat16)

        if j + SLOTS < units:
            load_g(j + SLOTS).start()
            load_u(j + SLOTS).start()
        goal = outs if j + SLOTS + 1 >= units else min(outs, issued + 1)
        while issued < goal:
            load_d(issued).start()
            issued += 1
    while issued < outs:
        load_d(issued).start()
        issued += 1

    relay_aux.wait_recv()
    expert = me // (devices // EXPERTS)
    spot = lax.broadcasted_iota(jnp.int32, (2 * rows, AUX), 1)
    hot = (spot == expert) | (spot == expert + EXPERTS)
    for half in range(2):
        @pl.loop(0, chips // 2)
        def _(b):
            pair = jnp.concatenate(
                [ax[half, 2 * b].astype(jnp.float32), ax[half, 2 * b + 1].astype(jnp.float32)], axis=0
            )
            at = pl.multiple_of(half * mates + b * 2 * rows, 2 * rows)
            total = jnp.sum(jnp.where(hot, pair, 0.0), axis=1, keepdims=True)
            share[pl.ds(at, 2 * rows), :] = jnp.broadcast_to(total, (2 * rows, AUX))

    def swap(c):
        return remote(mine.at[c, other], theirs.at[c], ob_send.at[c], ob_recv.at[c], peer)

    def give(c):
        swap(c).wait_recv()

        @pl.loop(0, chips // 2)
        def _(b):
            at = pl.multiple_of(b * 2 * rows, 2 * rows)
            both = mine[c, core, pl.ds(at, 2 * rows), :] + theirs[c, pl.ds(at, 2 * rows), :]
            sbuf[c, 2 * b] = both[:rows].astype(jnp.bfloat16)
            sbuf[c, 2 * b + 1] = both[rows:].astype(jnp.bfloat16)

        @pl.loop(1, chips)
        def _(i):
            dest = lax.rem(chip + i, chips)
            remote(
                sbuf.at[c, dest], rbuf.at[c, chip], rt_send.at[c], rt_recv.at[c], dest * 2 + core
            ).start()

        rbuf[c, chip] = sbuf[c, chip]

    sub = min(tile, nc)
    for c in range(outs):
        load_d(c).wait()

        @pl.loop(0, nc // sub, unroll=True)
        def _(n):
            cols = pl.ds(pl.multiple_of(n * sub, sub), sub)
            o = jnp.dot(hid[...], down[c, :, cols], preferred_element_type=jnp.float32)
            o = o * share[:, :1]
            mine[c, 0, :, cols] = o[:mates]
            mine[c, 1, :, cols] = o[mates:]

        swap(c).start()
        if c > 0:
            give(c - 1)
    give(outs - 1)

    for c in range(outs):
        many(rbuf.at[c, pl.ds(0, chips - 1)], rt_recv.at[c]).wait()
        total = rbuf[c, 0].astype(jnp.float32)
        if chips <= 16:
            for b in range(1, chips):
                total = total + rbuf[c, b].astype(jnp.float32)
        else:
            total = lax.fori_loop(1, chips, lambda b, t: t + rbuf[c, b].astype(jnp.float32), total)
        out[:, c * nc : (c + 1) * nc] = total.astype(jnp.bfloat16)

    for j in range(units):
        many(rx.at[j, 0, pl.ds(0, chips - 1)], tx_send.at[j]).wait()
        relay(j).wait_send()
    many(ax.at[0, pl.ds(0, chips - 1)], ax_send.at[0]).wait()
    relay_aux.wait_send()
    for c in range(outs):
        swap(c).wait_send()
        many(rbuf.at[c, pl.ds(0, chips - 1)], rt_send.at[c]).wait()


def layer(tokens, routes, gates, wg, wu, wd):
    devices = lax.axis_size("ep")
    rows, width = tokens.shape
    hidden = wg.shape[1]
    chips = devices // 2
    kc, nc = piece(width, 1024), piece(width, 1024)
    tile = piece(hidden, 512)
    units, outs = width // kc, width // nc
    batch = devices * rows
    bf16, f32 = jnp.bfloat16, jnp.float32
    dma = pltpu.SemaphoreType.DMA
    anywhere = pl.BlockSpec(memory_space=pl.ANY)
    vmem = pl.BlockSpec(memory_space=pltpu.VMEM)
    return pl.pallas_call(
        functools.partial(kernel, devices, kc, nc, tile),
        out_shape=jax.ShapeDtypeStruct((rows, width), bf16),
        in_specs=[anywhere, vmem, vmem, anywhere, anywhere, anywhere],
        out_specs=vmem,
        scratch_shapes=[
            pltpu.VMEM((SLOTS, kc, hidden), bf16),
            pltpu.VMEM((SLOTS, kc, hidden), bf16),
            pltpu.VMEM((outs, hidden, nc), bf16),
            pltpu.VMEM((units, 2, chips, rows, kc), bf16),
            pltpu.VMEM((2, chips, rows, AUX), bf16),
            pltpu.VMEM((batch, kc), f32),
            pltpu.VMEM((batch, kc), bf16),
            pltpu.VMEM((batch, hidden), f32),
            pltpu.VMEM((batch, hidden), f32),
            pltpu.VMEM((batch, hidden), bf16),
            pltpu.VMEM((batch, AUX), f32),
            pltpu.VMEM((outs, 2, chips * rows, nc), f32),
            pltpu.VMEM((outs, chips * rows, nc), f32),
            pltpu.VMEM((outs, chips, rows, nc), bf16),
            pltpu.VMEM((outs, chips, rows, nc), bf16),
            dma((units,)), dma((SLOTS,)), dma((SLOTS,)), dma((outs,)),
            dma((units,)), dma((units,)), dma((units,)), dma((units,)),
            dma((outs,)), dma((outs,)), dma((outs,)), dma((outs,)),
            dma((2,)), dma((2,)),
        ],
        compiler_params=pltpu.CompilerParams(
            collective_id=0, has_side_effects=True, vmem_limit_bytes=67_043_328
        ),
    )(tokens, routes, gates, wg, wu, wd)


def solution(mesh):
    placed = (
        P(("groups", "ep"), None),
        P(("groups", "ep"), None),
        P(("groups", "ep"), None),
        P(None, "ep"),
        P(None, "ep"),
        P("ep", None),
    )
    return jax.shard_map(
        layer, mesh=mesh, in_specs=placed, out_specs=P(("groups", "ep"), None), check_vma=False
    )
```

profile of v0, /device:TPU:0, one launch (start us, length us, event | category | flops | bytes accessed | tf_op | source)
XLA Modules:
  0.0 50.1 jit_solution(13197676122772791115)
XLA Ops:
  0.0 48.6 %shard_map.64 = bf16[4,7168]{1,0:T(4,128)(2,1)} custom-call(bf16[4,7168]{1,0:T(4,128)(2,1)} %tokens.1, s32[4,8]{1,0:T(4,128)} %routes.1, f32[4,8]{1,0:T(4,128)} %gates.1, bf16[7168,2048]{1,0:T(8,128)(2,1)} %wg.1, bf16[7168,2048]{1,0:T(8,128)(2,1)} %wu.1, bf16[2048,7168]{1,0:T(8,128)(2,1)} %wd.1), custom_call_target="tpu_custom_call" | custom-call | tf_op jit(solution)/shard_map/pallas_call | solution.py:249
  48.6 1.5 %copy.8 = bf16[4,7168]{1,0:T(4,128)(2,1)} copy(bf16[4,7168]{1,0:T(4,128)(2,1)} %shard_map.64) | data formatting | bytes 114688
where the time goes:
time: 50.2 us; the launch traced here: 50.1 us
  Pallas kernels  48.6 us (97%)
  local copies, waits for them, and re-layouts  1.46 us (3%)
    pallas_call x1, Pallas kernels, layer(): pl.pallas_call(functools.partial(kernel, devices, kc, nc, tile), out_shap...  48.6 us
    unnamed x1, local copies, waits for them, and re-layouts  1.46 us

commit v1 on v0

v1 whole, which is shorter than its diff:
```python
import functools

import jax
import jax.numpy as jnp
from jax import lax
from jax.experimental import pallas as pl
from jax.experimental.pallas import tpu as pltpu
from jax.sharding import PartitionSpec as P

EXPERTS = 16
SLOTS = 7
AHEAD = 2
AUX = 128


def piece(total, want):
    size = want
    while total % size:
        size //= 2
    return size


def split_chips(chips):
    inner = 1
    while inner * inner * 4 <= chips:
        inner *= 2
    return inner


def column_spans(width, big, small):
    spans, at = [], 0
    while at + big < width:
        spans.append((at, big))
        at += big
    for size in (big // 2, small, small):
        size = min(size, width - at)
        if size:
            spans.append((at, size))
            at += size
    return spans


def kernel(
    devices, inner, kc, spans, tile,
    tokens, routes, gates, wg, wu, wd, out,
    ring_g, ring_u, down, rx, ax, xb, acc_g, acc_u, hid, share, mine, theirs, own, xs, xr, zs, zr,
    tok_sem, g_sem, u_sem, d_sem,
    tz_send, tz_recv, tx_send, tx_recv, re_send, re_recv,
    ob_send, ob_recv, rx_send, rx_recv, rz_send, rz_recv, ax_send, ax_recv,
):
    rows, width = tokens.shape
    hidden = wg.shape[1]
    chips = devices // 2
    outer = chips // inner
    block = outer * rows
    slots = ring_g.shape[0]
    units, outs = width // kc, len(spans)
    me = lax.axis_index("ep")
    chip, core = me // 2, me % 2
    z, x = chip // inner, chip % inner
    other = 1 - core
    peer = chip * 2 + other
    line = (core * inner + x) * outer
    mates = chips * rows

    def place(to_z, to_x):
        return (to_z * inner + to_x) * 2 + core

    def along_z(i):
        return lax.rem(z + i, outer)

    def along_x(i):
        return lax.rem(x + i, inner)

    def remote(src, dst, send, recv, dev):
        return pltpu.make_async_remote_copy(
            src_ref=src, dst_ref=dst, send_sem=send, recv_sem=recv,
            device_id={"ep": dev}, device_id_type=pl.DeviceIdType.MESH,
        )

    def many(ref, sem):
        return pltpu.make_async_copy(ref, ref, sem)

    def load_tokens(j):
        return pltpu.make_async_copy(
            tokens.at[:, pl.ds(j * kc, kc)], rx.at[j, line + z], tok_sem.at[j]
        )

    def load_g(j):
        s = j % slots
        return pltpu.make_async_copy(wg.at[pl.ds(j * kc, kc), :], ring_g.at[s], g_sem.at[s])

    def load_u(j):
        s = j % slots
        return pltpu.make_async_copy(wu.at[pl.ds(j * kc, kc), :], ring_u.at[s], u_sem.at[s])

    def load_d(c):
        cols = pl.ds(*spans[c])
        return pltpu.make_async_copy(wd.at[:, cols], down.at[:, cols], d_sem.at[c])

    for j in range(units):
        load_tokens(j).start()
    for j in range(min(slots, units)):
        load_g(j).start()
        load_u(j).start()
    issued = min(AHEAD, outs)
    for c in range(issued):
        load_d(c).start(priority=1)

    barrier = pltpu.get_barrier_semaphore()

    def greet(dev):
        pl.semaphore_signal(barrier, inc=1, device_id={"ep": dev}, device_id_type=pl.DeviceIdType.MESH)

    for i in range(1, outer):
        greet(place(along_z(i), x))
    for i in range(1, inner):
        greet(place(z, along_x(i)))
    greet(peer)

    lane = lax.broadcasted_iota(jnp.int32, (rows, AUX), 1)
    name = jnp.where(lane < EXPERTS, lane, lane - EXPERTS)
    weight = jnp.zeros((rows, AUX), jnp.float32)
    for k in range(routes.shape[1]):
        weight = weight + jnp.where(routes[:, k : k + 1] == name, gates[:, k : k + 1], 0.0)
    high = weight.astype(jnp.bfloat16).astype(jnp.float32)
    ax[line + z] = jnp.where(
        lane < EXPERTS, high, jnp.where(lane < 2 * EXPERTS, weight - high, 0.0)
    ).astype(jnp.bfloat16)

    pl.semaphore_wait(barrier, outer + inner - 1)

    for j in range(units):
        load_tokens(j).wait()
        for i in range(1, outer):
            slot = rx.at[j, line + z]
            remote(slot, slot, tz_send.at[j], tz_recv.at[j], place(along_z(i), x)).start()
    for i in range(1, outer):
        slot = ax.at[line + z]
        remote(slot, slot, ax_send.at[0], ax_recv.at[0], place(along_z(i), x)).start()

    def hop_x(j):
        many(rx.at[j, pl.ds(0, outer - 1)], tz_recv.at[j]).wait()
        for i in range(1, inner):
            part = rx.at[j, pl.ds(line, outer)]
            remote(part, part, tx_send.at[j], tx_recv.at[j], place(z, along_x(i))).start()

    def relay(j):
        half = rx.at[j, pl.ds(core * chips, chips)]
        return remote(half, half, re_send.at[j], re_recv.at[j], peer)

    def hop_core(j):
        many(rx.at[j, pl.ds(0, chips - outer)], tx_recv.at[j]).wait()
        relay(j).start()

    half_ax = ax.at[pl.ds(core * chips, chips)]
    relay_aux = remote(half_ax, half_ax, ax_send.at[2], ax_recv.at[2], peer)

    lead = min(units, LEAD)
    ahead = min(units, LEAD2)
    for j in range(lead):
        hop_x(j)
    sent = 0
    for j in range(lead, units):
        hop_x(j)
        if sent < ahead:
            hop_core(sent)
            sent += 1
    many(ax.at[pl.ds(0, outer - 1)], ax_recv.at[0]).wait()
    for i in range(1, inner):
        part = ax.at[pl.ds(line, outer)]
        remote(part, part, ax_send.at[1], ax_recv.at[1], place(z, along_x(i))).start()

    group = max(1, 16 // rows)

    def gather_rows(j, b):
        parts = [rx[j, b * group + i].astype(jnp.float32) for i in range(group)]
        whole = parts[0] if group == 1 else jnp.concatenate(parts, axis=0)
        return whole.astype(jnp.bfloat16)

    for j in range(units):
        while sent < min(units, j + 1 + ahead):
            hop_core(sent)
            sent += 1
        relay(j).wait_recv()
        if devices // group <= 16:
            for b in range(devices // group):
                xb[b * group * rows : (b + 1) * group * rows, :] = gather_rows(j, b)
        else:
            @pl.loop(0, devices // group)
            def _(b):
                xb[pl.ds(pl.multiple_of(b * group * rows, group * rows), group * rows), :] = gather_rows(j, b)
        load_g(j).wait()
        load_u(j).wait()
        s = j % slots

        for n in range(hidden // tile):
            cols = pl.ds(n * tile, tile)
            pg = jnp.dot(xb[...], ring_g[s, :, cols], preferred_element_type=jnp.float32)
            pu = jnp.dot(xb[...], ring_u[s, :, cols], preferred_element_type=jnp.float32)
            if j == 0:
                acc_g[:, cols] = pg
                acc_u[:, cols] = pu
            elif j < units - 1:
                acc_g[:, cols] += pg
                acc_u[:, cols] += pu
            else:
                g = acc_g[:, cols] + pg
                u = acc_u[:, cols] + pu
                hid[:, cols] = (g / (1.0 + jnp.exp(-g)) * u).astype(jnp.bfloat16)

        if j + slots < units:
            load_g(j + slots).start()
            load_u(j + slots).start()
        if j + slots + 1 >= units:
            while issued < outs:
                load_d(issued).start(priority=1)
                issued += 1

    many(ax.at[pl.ds(0, chips - outer)], ax_recv.at[1]).wait()
    relay_aux.start()
    relay_aux.wait_recv()
    expert = me // (devices // EXPERTS)
    spot = lax.broadcasted_iota(jnp.int32, (group * rows, AUX), 1)
    hot = (spot == expert) | (spot == expert + EXPERTS)

    def share_rows(b):
        parts = [ax[b * group + i].astype(jnp.float32) for i in range(group)]
        whole = parts[0] if group == 1 else jnp.concatenate(parts, axis=0)
        total = jnp.sum(jnp.where(hot, whole, 0.0), axis=1, keepdims=True)
        return jnp.broadcast_to(total, (group * rows, AUX))

    if devices // group <= 16:
        for b in range(devices // group):
            share[b * group * rows : (b + 1) * group * rows, :] = share_rows(b)
    else:
        @pl.loop(0, devices // group)
        def _(b):
            share[pl.ds(pl.multiple_of(b * group * rows, group * rows), group * rows), :] = share_rows(b)

    def swap(c):
        cols = pl.ds(*spans[c])
        return remote(mine.at[other, :, cols], theirs.at[:, cols], ob_send.at[c], ob_recv.at[c], peer)

    def sum_core(c):
        cols = pl.ds(*spans[c])
        swap(c).wait_recv()
        for i in range(1, inner):
            to = along_x(i)
            at = pl.ds(pl.multiple_of(to * block, block), block)
            xs[to, :, cols] = (mine[core, at, cols] + theirs[at, cols]).astype(jnp.bfloat16)
            remote(
                xs.at[to, :, cols], xr.at[x, :, cols], rx_send.at[c], rx_recv.at[c], place(z, to)
            ).start()
        at = pl.ds(pl.multiple_of(x * block, block), block)
        own[:, cols] = mine[core, at, cols] + theirs[at, cols]

    def sum_x(c):
        cols = pl.ds(*spans[c])
        many(xr.at[pl.ds(0, inner - 1), :, cols], rx_recv.at[c]).wait()
        total = own[:, cols]
        for i in range(1, inner):
            total = total + xr[along_x(i), :, cols].astype(jnp.float32)
        for b in range(outer):
            zs[b, :, cols] = total[b * rows : (b + 1) * rows].astype(jnp.bfloat16)
        for i in range(1, outer):
            to = along_z(i)
            remote(
                zs.at[to, :, cols], zr.at[z, :, cols], rz_send.at[c], rz_recv.at[c], place(to, x)
            ).start()
        zr[z, :, cols] = zs[z, :, cols]

    def sum_z(c):
        cols = pl.ds(*spans[c])
        many(zr.at[pl.ds(0, outer - 1), :, cols], rz_recv.at[c]).wait()
        total = zr[0, :, cols].astype(jnp.float32)
        for b in range(1, outer):
            total = total + zr[b, :, cols].astype(jnp.float32)
        out[:, cols] = total.astype(jnp.bfloat16)

    stages = ((LAGS[0], sum_core), (LAGS[1], sum_x), (LAGS[2], sum_z))
    for c in range(outs + LAGS[2]):
        if c < outs:
            load_d(c).wait()
            at, size = spans[c]
            sub = min(tile, size)
            for n in range(size // sub):
                cols = pl.ds(at + n * sub, sub)
                o = jnp.dot(hid[...], down[:, cols], preferred_element_type=jnp.float32)
                o = o * share[:, :1]
                mine[0, :, cols] = o[:mates]
                mine[1, :, cols] = o[mates:]
            swap(c).start()
        for lag, stage in stages:
            if 0 <= c - lag < outs:
                stage(c - lag)

    for j in range(units):
        many(rx.at[j, pl.ds(0, outer - 1)], tz_send.at[j]).wait()
        many(rx.at[j, pl.ds(0, chips - outer)], tx_send.at[j]).wait()
        relay(j).wait_send()
    many(ax.at[pl.ds(0, outer - 1)], ax_send.at[0]).wait()
    many(ax.at[pl.ds(0, chips - outer)], ax_send.at[1]).wait()
    relay_aux.wait_send()
    for c in range(outs):
        cols = pl.ds(*spans[c])
        swap(c).wait_send()
        many(xr.at[pl.ds(0, inner - 1), :, cols], rx_send.at[c]).wait()
        many(zr.at[pl.ds(0, outer - 1), :, cols], rz_send.at[c]).wait()


LEAD, LEAD2 = 4, 3
LAGS = (1, 3, 6)


def layer(tokens, routes, gates, wg, wu, wd):
    devices = lax.axis_size("ep")
    rows, width = tokens.shape
    hidden = wg.shape[1]
    chips = devices // 2
    inner = split_chips(chips)
    outer = chips // inner
    kc = piece(width, 512)
    tile = piece(hidden, 512)
    spans = column_spans(width, piece(width, 1024), 256)
    units, outs = width // kc, len(spans)
    slots = min(SLOTS, units)
    batch = devices * rows
    bf16, f32 = jnp.bfloat16, jnp.float32
    dma = pltpu.SemaphoreType.DMA
    anywhere = pl.BlockSpec(memory_space=pl.ANY)
    vmem = pl.BlockSpec(memory_space=pltpu.VMEM)
    return pl.pallas_call(
        functools.partial(kernel, devices, inner, kc, spans, tile),
        out_shape=pltpu.VMEM((rows, width), bf16),
        in_specs=[anywhere, vmem, vmem, anywhere, anywhere, anywhere],
        out_specs=vmem,
        scratch_shapes=[
            pltpu.VMEM((slots, kc, hidden), bf16),
            pltpu.VMEM((slots, kc, hidden), bf16),
            pltpu.VMEM((hidden, width), bf16),
            pltpu.VMEM((units, devices, rows, kc), bf16),
            pltpu.VMEM((devices, rows, AUX), bf16),
            pltpu.VMEM((batch, kc), bf16),
            pltpu.VMEM((batch, hidden), f32),
            pltpu.VMEM((batch, hidden), f32),
            pltpu.VMEM((batch, hidden), bf16),
            pltpu.VMEM((batch, AUX), f32),
            pltpu.VMEM((2, chips * rows, width), f32),
            pltpu.VMEM((chips * rows, width), f32),
            pltpu.VMEM((outer * rows, width), f32),
            pltpu.VMEM((inner, outer * rows, width), bf16),
            pltpu.VMEM((inner, outer * rows, width), bf16),
            pltpu.VMEM((outer, rows, width), bf16),
            pltpu.VMEM((outer, rows, width), bf16),
            dma((units,)), dma((slots,)), dma((slots,)), dma((outs,)),
            dma((units,)), dma((units,)), dma((units,)), dma((units,)), dma((units,)), dma((units,)),
            dma((outs,)), dma((outs,)), dma((outs,)), dma((outs,)), dma((outs,)), dma((outs,)),
            dma((3,)), dma((3,)),
        ],
        compiler_params=pltpu.CompilerParams(
            collective_id=0, has_side_effects=True, vmem_limit_bytes=66_800_000
        ),
    )(tokens, routes, gates, wg, wu, wd)


def solution(mesh):
    placed = (
        P(("groups", "ep"), None),
        P(("groups", "ep"), None),
        P(("groups", "ep"), None),
        P(None, "ep"),
        P(None, "ep"),
        P("ep", None),
    )
    return jax.shard_map(
        layer, mesh=mesh, in_specs=placed, out_specs=P(("groups", "ep"), None), check_vma=False
    )
```

time: 50.2 us -> 47.5 us (0.946)
  Pallas kernels: 48.6 us -> 46.7 us
  local copies, waits for them, and re-layouts: 1.46 us -> 0.63 us
    pallas_call x1, Pallas kernels: 48.6 us -> 46.7 us  [layer(): pl.pallas_call(functools.partial(kernel, devices, inner, kc, spans, tile)...]
    unnamed x1, local copies, waits for them, and re-layouts: 1.46 us -> 0.63 us
where the time goes in v1:
time: 47.5 us; the launch traced here: 47.4 us
  Pallas kernels  46.7 us (98%)
  local copies, waits for them, and re-layouts  0.63 us (1%)
    pallas_call x1, Pallas kernels, layer(): pl.pallas_call(functools.partial(kernel, devices, inner, kc, spans, tile)...  46.7 us

profile of v1, /device:TPU:0, one launch (start us, length us, event | category | flops | bytes accessed | tf_op | source)
XLA Modules:
  0.0 47.4 jit_solution(3050267338014251353)
XLA Ops:
  0.0 46.7 %shard_map.64 = bf16[4,7168]{1,0:T(4,128)(2,1)S(1)} custom-call(bf16[4,7168]{1,0:T(4,128)(2,1)} %tokens.1, s32[4,8]{1,0:T(4,128)} %routes.1, f32[4,8]{1,0:T(4,128)} %gates.1, bf16[7168,2048]{1,0:T(8,128)(2,1)} %wg.1, bf16[7168,2048]{1,0:T(8,128)(2,1)} %wu.1, bf16[2048,7168]{1,0:T(8,128)(2,1)} %wd.1), custom_call_target="tpu_custom_call" | custom-call | tf_op jit(solution)/shard_map/pallas_call | solution.py:333
  46.8 0.6 %copy.8 = bf16[4,7168]{1,0:T(4,128)(2,1)} copy(bf16[4,7168]{1,0:T(4,128)(2,1)S(1)} %shard_map.64) | data formatting | bytes 114688

commit v2 on v1

--- a/solution.py
+++ b/solution.py
@@ -9,7 +9,12 @@
 
 EXPERTS = 16
 SLOTS = 7
-AHEAD = 2
+AHEAD = 1
+WINDOW = 5
+LEAD, LEAD2 = 4, 3
+LAGS = (1, 4, 8)
+TAIL = [512, 256, 256]
+DIRECT = 1
 AUX = 128
 
 
@@ -27,23 +32,19 @@
     return inner
 
 
-def column_spans(width, big, small):
-    spans, at = [], 0
-    while at + big < width:
-        spans.append((at, big))
-        at += big
-    for size in (big // 2, small, small):
-        size = min(size, width - at)
-        if size:
-            spans.append((at, size))
-            at += size
-    return spans
+def column_spans(width, big):
+    sizes, left = [], width - sum(TAIL)
+    while left:
+        sizes.append(min(big, left))
+        left -= sizes[-1]
+    sizes += TAIL
+    return [(sum(sizes[:i]), size) for i, size in enumerate(sizes)]
 
 
 def kernel(
     devices, inner, kc, spans, tile,
     tokens, routes, gates, wg, wu, wd, out,
-    ring_g, ring_u, down, rx, ax, xb, acc_g, acc_u, hid, share, mine, theirs, own, xs, xr, zs, zr,
+    ring_g, ring_u, down, rx, ax, xb, acc_g, acc_u, hid, share, mine, theirs, own, xs, xr, zs, zr, ds, dr,
     tok_sem, g_sem, u_sem, d_sem,
     tz_send, tz_recv, tx_send, tx_recv, re_send, re_recv,
     ob_send, ob_recv, rx_send, rx_recv, rz_send, rz_recv, ax_send, ax_recv,
@@ -101,21 +102,16 @@
     for j in range(units):
         load_tokens(j).start()
     for j in range(min(slots, units)):
-        load_g(j).start()
-        load_u(j).start()
-    issued = min(AHEAD, outs)
-    for c in range(issued):
-        load_d(c).start(priority=1)
+        load_g(j).start(priority=1)
+        load_u(j).start(priority=1)
 
     barrier = pltpu.get_barrier_semaphore()
 
     def greet(dev):
         pl.semaphore_signal(barrier, inc=1, device_id={"ep": dev}, device_id_type=pl.DeviceIdType.MESH)
 
-    for i in range(1, outer):
-        greet(place(along_z(i), x))
-    for i in range(1, inner):
-        greet(place(z, along_x(i)))
+    for i in range(1, chips):
+        greet(lax.rem(chip + i, chips) * 2 + core)
     greet(peer)
 
     lane = lax.broadcasted_iota(jnp.int32, (rows, AUX), 1)
@@ -128,7 +124,7 @@
         lane < EXPERTS, high, jnp.where(lane < 2 * EXPERTS, weight - high, 0.0)
     ).astype(jnp.bfloat16)
 
-    pl.semaphore_wait(barrier, outer + inner - 1)
+    pl.semaphore_wait(barrier, chips)
 
     for j in range(units):
         load_tokens(j).wait()
@@ -178,6 +174,18 @@
         whole = parts[0] if group == 1 else jnp.concatenate(parts, axis=0)
         return whole.astype(jnp.bfloat16)
 
+    issued, waited = 0, 0
+
+    def feed(others, least=0):
+        nonlocal issued
+        while issued < outs and (
+            issued < least
+            or others + hidden * sum(n for _, n in spans[waited : issued + 1]) <= WINDOW * 2 * kc * hidden
+        ):
+            load_d(issued).start(priority=1)
+            issued += 1
+
+    feed(units * 2 * kc * hidden, AHEAD)
     for j in range(units):
         while sent < min(units, j + 1 + ahead):
             hop_core(sent)
@@ -210,12 +218,9 @@
                 hid[:, cols] = (g / (1.0 + jnp.exp(-g)) * u).astype(jnp.bfloat16)
 
         if j + slots < units:
-            load_g(j + slots).start()
-            load_u(j + slots).start()
-        if j + slots + 1 >= units:
-            while issued < outs:
-                load_d(issued).start(priority=1)
-                issued += 1
+            load_g(j + slots).start(priority=1)
+            load_u(j + slots).start(priority=1)
+        feed(kc * 2 * hidden * max(0, min(units, j + 1 + slots) - j - 1))
 
     many(ax.at[pl.ds(0, chips - outer)], ax_recv.at[1]).wait()
     relay_aux.start()
@@ -278,10 +283,53 @@
             total = total + zr[b, :, cols].astype(jnp.float32)
         out[:, cols] = total.astype(jnp.bfloat16)
 
-    stages = ((LAGS[0], sum_core), (LAGS[1], sum_x), (LAGS[2], sum_z))
+    near = spans[outs - DIRECT][0]
+
+    def give(c):
+        at, size = spans[c]
+        cols, mine_at = pl.ds(at, size), pl.ds(at - near, size)
+        swap(c).wait_recv()
+        both = mine[core, :, cols] + theirs[:, cols]
+        for b in range(chips):
+            ds[b % outer * inner + b // outer, :, mine_at] = both[b * rows : (b + 1) * rows].astype(jnp.bfloat16)
+        for i in range(1, chips):
+            to = lax.rem(chip + i, chips)
+            remote(
+                ds.at[to, :, mine_at], dr.at[chip, :, mine_at], rz_send.at[c], rz_recv.at[c], to * 2 + core
+            ).start()
+        dr[chip, :, mine_at] = ds[chip, :, mine_at]
+
+    def sum_all(c):
+        at, size = spans[c]
+        cols, mine_at = pl.ds(at, size), pl.ds(at - near, size)
+        many(dr.at[pl.ds(0, chips - 1), :, mine_at], rz_recv.at[c]).wait()
+        total = dr[0, :, mine_at].astype(jnp.float32)
+        for b in range(1, chips):
+            total = total + dr[b, :, mine_at].astype(jnp.float32)
+        out[:, cols] = total.astype(jnp.bfloat16)
+
+    def stage_1(c):
+        if c < outs - DIRECT:
+            sum_core(c)
+        else:
+            give(c)
+
+    def stage_2(c):
+        if c < outs - DIRECT:
+            sum_x(c)
+
+    def stage_3(c):
+        if c < outs - DIRECT:
+            sum_z(c)
+        else:
+            sum_all(c)
+
+    stages = ((LAGS[0], stage_1), (LAGS[1], stage_2), (LAGS[2], stage_3))
     for c in range(outs + LAGS[2]):
         if c < outs:
             load_d(c).wait()
+            waited += 1
+            feed(0)
             at, size = spans[c]
             sub = min(tile, size)
             for n in range(size // sub):
@@ -305,12 +353,12 @@
     for c in range(outs):
         cols = pl.ds(*spans[c])
         swap(c).wait_send()
-        many(xr.at[pl.ds(0, inner - 1), :, cols], rx_send.at[c]).wait()
-        many(zr.at[pl.ds(0, outer - 1), :, cols], rz_send.at[c]).wait()
-
-
-LEAD, LEAD2 = 4, 3
-LAGS = (1, 3, 6)
+        if c < outs - DIRECT:
+            many(xr.at[pl.ds(0, inner - 1), :, cols], rx_send.at[c]).wait()
+            many(zr.at[pl.ds(0, outer - 1), :, cols], rz_send.at[c]).wait()
+        else:
+            cols = pl.ds(spans[c][0] - near, spans[c][1])
+            many(dr.at[pl.ds(0, chips - 1), :, cols], rz_send.at[c]).wait()
 
 
 def layer(tokens, routes, gates, wg, wu, wd):
@@ -322,7 +370,8 @@
     outer = chips // inner
     kc = piece(width, 512)
     tile = piece(hidden, 512)
-    spans = column_spans(width, piece(width, 1024), 256)
+    spans = column_spans(width, 1024)
+    near = spans[len(spans) - DIRECT][0]
     units, outs = width // kc, len(spans)
     slots = min(SLOTS, units)
     batch = devices * rows
@@ -348,11 +397,13 @@
             pltpu.VMEM((batch, AUX), f32),
             pltpu.VMEM((2, chips * rows, width), f32),
             pltpu.VMEM((chips * rows, width), f32),
-            pltpu.VMEM((outer * rows, width), f32),
-            pltpu.VMEM((inner, outer * rows, width), bf16),
-            pltpu.VMEM((inner, outer * rows, width), bf16),
-            pltpu.VMEM((outer, rows, width), bf16),
-            pltpu.VMEM((outer, rows, width), bf16),
+            pltpu.VMEM((outer * rows, near), f32),
+            pltpu.VMEM((inner, outer * rows, near), bf16),
+            pltpu.VMEM((inner, outer * rows, near), bf16),
+            pltpu.VMEM((outer, rows, near), bf16),
+            pltpu.VMEM((outer, rows, near), bf16),
+            pltpu.VMEM((chips, rows, width - near), bf16),
+            pltpu.VMEM((chips, rows, width - near), bf16),
             dma((units,)), dma((slots,)), dma((slots,)), dma((outs,)),
             dma((units,)), dma((units,)), dma((units,)), dma((units,)), dma((units,)), dma((units,)),
             dma((outs,)), dma((outs,)), dma((outs,)), dma((outs,)), dma((outs,)), dma((outs,)),

time: 47.5 us -> 43.4 us (0.914)
  Pallas kernels: 46.7 us -> 42.6 us
    pallas_call x1, Pallas kernels: 46.7 us -> 42.6 us  [layer(): pl.pallas_call(functools.partial(kernel, devices, inner, kc, spans, tile)...]
where the time goes in v2:
time: 43.4 us; the launch traced here: 43.2 us
  Pallas kernels  42.6 us (98%)
  local copies, waits for them, and re-layouts  0.63 us (1%)
    pallas_call x1, Pallas kernels, layer(): pl.pallas_call(functools.partial(kernel, devices, inner, kc, spans, tile)...  42.6 us

profile of v2, /device:TPU:0, one launch (start us, length us, event | category | flops | bytes accessed | tf_op | source)
XLA Modules:
  0.0 43.2 jit_solution(15157108002759653411)
XLA Ops:
  0.0 42.6 %shard_map.64 = bf16[4,7168]{1,0:T(4,128)(2,1)S(1)} custom-call(bf16[4,7168]{1,0:T(4,128)(2,1)} %tokens.1, s32[4,8]{1,0:T(4,128)} %routes.1, f32[4,8]{1,0:T(4,128)} %gates.1, bf16[7168,2048]{1,0:T(8,128)(2,1)} %wg.1, bf16[7168,2048]{1,0:T(8,128)(2,1)} %wu.1, bf16[2048,7168]{1,0:T(8,128)(2,1)} %wd.1), custom_call_target="tpu_custom_call" | custom-call | tf_op jit(solution)/shard_map/pallas_call | solution.py:382
  42.6 0.6 %copy.8 = bf16[4,7168]{1,0:T(4,128)(2,1)} copy(bf16[4,7168]{1,0:T(4,128)(2,1)S(1)} %shard_map.64) | data formatting | bytes 114688

commit v3 on v2

--- a/solution.py
+++ b/solution.py
@@ -12,9 +12,9 @@
 AHEAD = 1
 WINDOW = 5
 LEAD, LEAD2 = 4, 3
-LAGS = (1, 4, 8)
-TAIL = [512, 256, 256]
-DIRECT = 1
+LAGS = (1, 4, 10)
+TAIL = [512, 512, 256, 256]
+DIRECT = 3
 AUX = 128
 
 
@@ -99,20 +99,20 @@
         cols = pl.ds(*spans[c])
         return pltpu.make_async_copy(wd.at[:, cols], down.at[:, cols], d_sem.at[c])
 
+    barrier = pltpu.get_barrier_semaphore()
+
+    def greet(dev):
+        pl.semaphore_signal(barrier, inc=1, device_id={"ep": dev}, device_id_type=pl.DeviceIdType.MESH)
+
+    for i in range(1, chips):
+        greet(lax.rem(chip + i, chips) * 2 + core)
+    greet(peer)
+
     for j in range(units):
         load_tokens(j).start()
     for j in range(min(slots, units)):
         load_g(j).start(priority=1)
         load_u(j).start(priority=1)
-
-    barrier = pltpu.get_barrier_semaphore()
-
-    def greet(dev):
-        pl.semaphore_signal(barrier, inc=1, device_id={"ep": dev}, device_id_type=pl.DeviceIdType.MESH)
-
-    for i in range(1, chips):
-        greet(lax.rem(chip + i, chips) * 2 + core)
-    greet(peer)
 
     lane = lax.broadcasted_iota(jnp.int32, (rows, AUX), 1)
     name = jnp.where(lane < EXPERTS, lane, lane - EXPERTS)

time: 43.4 us -> 42.8 us (0.986)
  Pallas kernels: 42.6 us -> 42 us
    pallas_call x1, Pallas kernels: 42.6 us -> 42 us  [layer(): pl.pallas_call(functools.partial(kernel, devices, inner, kc, spans, tile)...]
where the time goes in v3:
time: 42.8 us; the launch traced here: 42.7 us
  Pallas kernels  42 us (98%)
  local copies, waits for them, and re-layouts  0.63 us (1%)
    pallas_call x1, Pallas kernels, layer(): pl.pallas_call(functools.partial(kernel, devices, inner, kc, spans, tile)...  42 us

profile of v3, /device:TPU:0, one launch (start us, length us, event | category | flops | bytes accessed | tf_op | source)
XLA Modules:
  0.0 42.7 jit_solution(4917724152885772997)
XLA Ops:
  0.0 42.0 %shard_map.64 = bf16[4,7168]{1,0:T(4,128)(2,1)S(1)} custom-call(bf16[4,7168]{1,0:T(4,128)(2,1)} %tokens.1, s32[4,8]{1,0:T(4,128)} %routes.1, f32[4,8]{1,0:T(4,128)} %gates.1, bf16[7168,2048]{1,0:T(8,128)(2,1)} %wg.1, bf16[7168,2048]{1,0:T(8,128)(2,1)} %wu.1, bf16[2048,7168]{1,0:T(8,128)(2,1)} %wd.1), custom_call_target="tpu_custom_call" | custom-call | tf_op jit(solution)/shard_map/pallas_call | solution.py:382
  42.0 0.6 %copy.8 = bf16[4,7168]{1,0:T(4,128)(2,1)} copy(bf16[4,7168]{1,0:T(4,128)(2,1)S(1)} %shard_map.64) | data formatting | bytes 114688
